TPU v7x, 128 devices: a whole 4x4x4 slice. The times are simulated.
128 devices in a mesh: dp: 16 (over z, y), tp: 8 (over x, core).
Axes of the slice: x: 4, y: 4, z: 4, core: 2. Of those that a mesh axis runs over, the one named last changes fastest.
Arguments:
- hidden: bfloat16 [1024, 4096], P(('dp', 'tp'))
- w_unembed: bfloat16 [4096, 131072], P(('dp', 'tp'))
Outputs:
- output: bfloat16 [1024, 131072], P(None, ('dp', 'tp'))
All inputs are finite; a program needn't handle non-finite values.
Results may differ from a plain program's by a relative error of at most 0.001.
Values are sent between devices in bfloat16 or wider.
A program may use at most 1 GiB of HBM per device.

v0:
```python
import jax
import jax.numpy as jnp
from jax import lax
from jax.sharding import PartitionSpec as P, NamedSharding


def solution(mesh):
    outer_size = mesh.shape["dp"]
    inner_size = mesh.shape["tp"]

    def local_part(hid_blk, w_blk):
        full_hidden = lax.all_gather(hid_blk, ("dp", "tp"), axis=0, tiled=True)
        rows_loc, vocab_size = w_blk.shape
        col_width = vocab_size // (outer_size * inner_size)
        w_split = w_blk.reshape(rows_loc, outer_size, inner_size, col_width)
        w_step = lax.all_to_all(w_split, "tp", 2, 0, tiled=True)
        w_cols = lax.all_to_all(w_step, "dp", 1, 0, tiled=True)
        w_cols = w_cols.reshape(outer_size * inner_size * rows_loc, col_width)
        return jnp.dot(full_hidden, w_cols, preferred_element_type=jnp.float32).astype(jnp.bfloat16)

    return jax.shard_map(
        local_part,
        mesh=mesh,
        in_specs=(P(("dp", "tp"), None), P(("dp", "tp"), None)),
        out_specs=P(None, ("dp", "tp")),
        check_vma=False,
    )
```

profile of v0, /device:TPU:1, one launch (start us, length us, event | category | flops | bytes accessed | tf_op | source)
XLA Modules:
  0.0 305.3 jit_solution(2441893764296878864)
XLA Ops:
  6.5 0.0 all-gather.2.cloned.1.call-start
  6.5 0.7 all-gather.2.cloned.1.call-update
  7.3 11.4 %copy.10 = bf16[4,8,128,1024]{3,2,1,0:T(8,128)(2,1)} copy(bf16[4,8,128,1024]{3,1,2,0:T(8,128)(2,1)} %bitcast.19) | data formatting | bytes 16777216
  18.6 11.3 %copy.6 = bf16[32,16,8,1024]{3,1,0,2:T(8,128)(2,1)} copy(bf16[32,16,8,1024]{3,2,1,0:T(8,128)(2,1)} %bitcast.18) | data formatting | bytes 16777216 | tf_op jit(solution)/shard_map/reshape | solution.py:15
  29.9 114.2 %all_to_all.33 = bf16[32,16,8,1024]{3,1,0,2:T(8,128)(2,1)} all-to-all(bf16[32,16,8,1024]{3,1,0,2:T(8,128)(2,1)} %copy.6), channel_id=1, replica_groups=mesh['dp'=16,'tp'=8] {'tp'}, dimensions={2} | all-to-all | bytes 16777216 | tf_op jit(solution)/shard_map/all_to_all | solution.py:16
  144.1 11.3 %copy.7 = bf16[256,16,1,1024]{3,0,2,1:T(8,128)(2,1)} copy(bf16[256,16,1,1024]{3,1,0,2:T(8,128)(2,1)} %bitcast.16) | data formatting | bytes 16777216 | tf_op jit(solution)/shard_map/all_to_all | solution.py:16
  155.4 105.8 %all_to_all.34 = bf16[256,16,1,1024]{3,0,2,1:T(8,128)(2,1)} all-to-all(bf16[256,16,1,1024]{3,0,2,1:T(8,128)(2,1)} %copy.7), channel_id=1, replica_groups=mesh['dp'=16,'tp'=8] {'dp'}, dimensions={1} | all-to-all | bytes 16777216 | tf_op jit(solution)/shard_map/all_to_all | solution.py:17
  261.2 11.3 %copy.12 = bf16[256,16,1,1024]{3,1,0,2:T(8,128)(2,1)} copy(bf16[256,16,1,1024]{3,0,2,1:T(8,128)(2,1)} %all_to_all.34) | data formatting | bytes 16777216 | tf_op jit(solution)/shard_map/all_to_all | solution.py:17
  272.5 11.3 %copy.9 = bf16[16,256,1,1,1024]{4,1,0,3,2:T(8,128)(2,1)} copy(bf16[16,256,1,1,1024]{4,0,1,3,2:T(8,128)(2,1)} %bitcast.17) | data formatting | bytes 16777216 | tf_op jit(solution)/shard_map/all_to_all | solution.py:17
  283.8 0.0 all-gather.2.cloned.1.call-done
  283.8 14.6 %convolution_convert_fusion = bf16[1024,1024]{1,0:T(8,128)(2,1)} fusion(bf16[1024,4096]{1,0:T(8,128)(2,1)} %all-gather.2.cloned.1.call-done, bf16[4096,1024]{1,0:T(8,128)(2,1)} %bitcast.20), kind=kOutput, calls=%fused_computation.1 | convolution fusion | flops 8590983168 | bytes 18874368 | tf_op jit(solution)/shard_map/dot_general | solution.py:19
Async XLA Ops:
  6.5 277.3 %all-gather.2.cloned.1.call-start = ((), (), s32[]{:S(2)}) async-start(), calls=%async_computation.2 | async-start | bytes 8454144 | tf_op jit(solution)/shard_map/all_gather | solution.py:12
Sparse Core Ops, SparseCore 0:
  10.3 95.5 all-gather.1
where the time goes:
time: 310 us; the launch traced here: 305 us
  blocking collectives  220 us (71%)
  local copies, waits for them, and re-layouts  56.6 us (18%)
  matrix products  14.6 us (5%)
  between operations  13.4 us (4%)
    all_to_all x1, blocking collectives, local_part(): w_step = lax.all_to_all(w_split, 'tp', 2, 0, tiled=True)  114 us
    all_to_all x1, blocking collectives, local_part(): w_cols = lax.all_to_all(w_step, 'dp', 1, 0, tiled=True)  106 us
    all_to_all x2, local copies, waits for them, and re-layouts, local_part(): w_cols = lax.all_to_all(w_step, 'dp', 1, 0, tiled=True)  22.6 us
    dot_general x1, matrix products, local_part(): jnp.dot(full_hidden, w_cols, preferred_element_type=jnp.float32)  14.6 us
    unnamed x1, local copies, waits for them, and re-layouts  11.4 us
    all_to_all x1, local copies, waits for them, and re-layouts, local_part(): w_step = lax.all_to_all(w_split, 'tp', 2, 0, tiled=True)  11.3 us
    reshape x1, local copies, waits for them, and re-layouts, local_part(): w_split = w_blk.reshape(rows_loc, outer_size, inner_size, col_width)  11.3 us
  transfers between devices with their start and end apart: 1, of which 0 were waited for; matrix products, arithmetic and copies ran while one was open for 19% of the time, Pallas kernels for 0%

commit v1 on v0

v1 whole, which is shorter than its diff:
```python
import functools

import jax
import jax.numpy as jnp
from jax import lax
from jax.experimental import pallas as pl
from jax.experimental.pallas import tpu as pltpu
from jax.sharding import PartitionSpec as P

MESH = pl.DeviceIdType.MESH
Z, Y, X = 0, 1, 2


def _turn(v):
    return (v[2], v[0], v[1])


def _neg(v):
    return tuple(-t % 4 for t in v)


def _routes():
    routes = {}
    for v in [(a, b, c) for a in range(4) for b in range(4) for c in range(4)]:
        if v == (0, 0, 0):
            continue
        w, order = v, (Z, Y, X)
        for _ in range(3):
            for u in (w, _neg(w)):
                if u not in routes:
                    routes[u] = tuple(a for a in order if u[a])
            w, order = _turn(w), tuple((a + 1) % 3 for a in order)
    routes[(1, 1, 1)], routes[(2, 2, 2)], routes[(3, 3, 3)] = (Z, Y, X), (Y, X, Z), (X, Z, Y)
    return routes


def _orbits(offsets):
    seen, groups = set(), []
    for v in offsets:
        if v in seen:
            continue
        group, w = [], v
        for _ in range(3):
            for u in (w, _neg(w)):
                if u not in seen:
                    seen.add(u)
                    group.append(u)
            w = _turn(w)
        groups.append(group)
    return groups


ROUTES = _routes()
THREE = _orbits([v for v in ROUTES if len(ROUTES[v]) == 3])
TWO = _orbits([v for v in ROUTES if len(ROUTES[v]) == 2])
ONE = [v for v in ROUTES if len(ROUTES[v]) == 1]
THREE_FLAT = [v for g in THREE for v in g]
TWO_FLAT = [v for g in TWO for v in g]
FIRST = THREE_FLAT + TWO_FLAT
PORTIONS = (((X, Y, Z), 0, 1408), ((Y, Z, X), 1408, 1408), ((Z, X, Y), 2816, 1280))


def _kernel(hid_ref, w_ref, out_ref, hbuf, wbuf, st_a, st_b, acc, r_a, r_b, r_k, s_w, r_h, s_h, r_x, s_x, l_sem):
    dp, tp = lax.axis_index("dp"), lax.axis_index("tp")
    pos, core = (dp // 4, dp % 4, tp // 2), tp % 2

    def shift(v):
        return tuple((p + d) % 4 if d else p for p, d in zip(pos, v))

    def dev(p, c):
        return (p[Z] * 4 + p[Y], p[X] * 2 + c)

    def chip(p):
        return (p[Z] * 4 + p[Y]) * 4 + p[X]

    def unit(axis, d):
        return tuple(d if a == axis else 0 for a in range(3))

    def send(src, dst, ssem, rsem, to):
        pltpu.make_async_remote_copy(
            src_ref=src, dst_ref=dst, send_sem=ssem, recv_sem=rsem, device_id=to, device_id_type=MESH
        ).start()

    def wait(ref, sem):
        pltpu.make_async_copy(ref, ref, sem).wait()

    barrier = pltpu.get_barrier_semaphore()
    peers = [dev(pos, 1 - core)]
    for axis in (X, Y, Z):
        for d in (1, 3, 2):
            for c in (core, 1 - core):
                peers.append(dev(shift(unit(axis, d)), c))
    for peer in peers:
        pl.semaphore_signal(barrier, inc=1, device_id=peer, device_id_type=MESH)
    pl.semaphore_wait(barrier, len(peers))

    def rows(slot, n=1):
        return pl.ds(pl.multiple_of(slot * 8, 8), n * 8)

    def runs(free, owner):
        out = []
        for z in range(4) if Z in free else (owner[Z],):
            for y in range(4) if Y in free and not (Y in free and X in free) else (owner[Y],):
                if X in free and Y in free:
                    out.append((core * 64 + z * 16, 16))
                elif X in free:
                    out.append((core * 64 + (z * 4 + y) * 4, 4))
                else:
                    out.append((core * 64 + (z * 4 + y) * 4 + owner[X], 1))
        return out

    def halves(part, col, width):
        if len(part) == 1 and part[0][1] == 1:
            cut = (width // 2 + 127) // 128 * 128
            s = part[0][0]
            return [(s, 1, col, cut)], [(s, 1, col + cut, width - cut)]
        if len(part) == 1:
            s, n = part[0]
            return [(s, n // 2, col, width)], [(s + n // 2, n // 2, col, width)]
        m = len(part) // 2
        return [(s, n, col, width) for s, n in part[:m]], [(s, n, col, width) for s, n in part[m:]]

    def sem_h(p, phase, step, side):
        return r_h.at[((p * 3 + phase) * 2 + step) * 2 + side]

    def hidden_send(phase, step):
        for p, (order, col, width) in enumerate(PORTIONS):
            axis, free = order[phase], order[:phase]
            for side, d in enumerate((1, 3)):
                to = dev(shift(unit(axis, d)), core)
                if step == 0:
                    items = [(s, n, col, width) for s, n in runs(free, pos)]
                else:
                    items = halves(runs(free, shift(unit(axis, 4 - d))), col, width)[side]
                for s, n, c0, cw in items:
                    dst = hbuf.at[rows(s, n), pl.ds(c0, cw)]
                    src = hid_ref.at[:, pl.ds(c0, cw)] if phase == 0 and step == 0 else dst
                    send(src, dst, s_h.at[p], sem_h(p, phase, step, side), to)

    def hidden_wait(phase, step):
        for p, (order, col, width) in enumerate(PORTIONS):
            n = 4**phase
            for side in range(2):
                if step == 0:
                    ref = hbuf.at[pl.ds(0, n * 8), pl.ds(col, width)]
                elif phase == 0:
                    cut = (width // 2 + 127) // 128 * 128
                    ref = hbuf.at[pl.ds(0, 8), pl.ds(col, cut if side == 0 else width - cut)]
                else:
                    ref = hbuf.at[pl.ds(0, n * 4), pl.ds(col, width)]
                wait(ref, sem_h(p, phase, step, side))

    def columns(c, n):
        return pl.ds(pl.multiple_of(c * 1024, 1024), n * 1024)

    def first_hop(v):
        i = FIRST.index(v)
        to = shift(unit(ROUTES[v][0], v[ROUTES[v][0]]))
        send(w_ref.at[:, columns(chip(shift(v)) * 2, 2)], st_a.at[i], s_w.at[0], r_a.at[i], dev(to, core))

    def deliver(src_of, v, last):
        axis, d = last
        to = shift(unit(axis, d))
        origin = tuple((t - o) % 4 for t, o in zip(to, v))
        at = wbuf.at[pl.ds(pl.multiple_of((chip(origin) * 2 + core) * 32, 32), 32)]
        for c in range(2):
            send(src_of(c), at, s_w.at[2], r_k.at[v[Z] * 4 + v[Y]], dev(to, c))

    def second_hop(v):
        i = FIRST.index(v)
        wait(st_a.at[i], r_a.at[i])
        axis = ROUTES[v][1]
        if len(ROUTES[v]) == 2:
            deliver(lambda c: st_a.at[i, :, pl.ds(c * 1024, 1024)], v, (axis, v[axis]))
        else:
            j = THREE_FLAT.index(v)
            send(st_a.at[i], st_b.at[j], s_w.at[1], r_b.at[j], dev(shift(unit(axis, v[axis])), core))

    def third_hop(v):
        j = THREE_FLAT.index(v)
        wait(st_b.at[j], r_b.at[j])
        axis = ROUTES[v][2]
        deliver(lambda c: st_b.at[j, :, pl.ds(c * 1024, 1024)], v, (axis, v[axis]))

    me = chip(pos) * 2 + core
    mine = wbuf.at[pl.ds(pl.multiple_of(me * 32, 32), 32)]
    slot = hbuf.at[rows(core * 64 + chip(pos))]
    pltpu.make_async_copy(hid_ref, slot, l_sem).start()
    pltpu.make_async_copy(w_ref.at[:, columns(me, 1)], mine, r_k.at[0]).start()

    fill = [[v for v in g] for g in THREE]
    batches = [fill[0], fill[1], fill[2], fill[3], [v for g in fill[4:] for v in g]]
    n = 0
    for phase in range(3):
        for step in range(2):
            hidden_send(phase, step)
            if n < len(batches):
                for v in batches[n]:
                    first_hop(v)
            n += 1
            if phase == 0 and step == 0:
                wait(slot, l_sem)
            if phase == 2:
                for g in TWO[:2] if step == 0 else TWO[2:]:
                    for v in g:
                        first_hop(v)
            if (phase, step) != (2, 1):
                hidden_wait(phase, step)
    send(w_ref.at[:, columns(chip(pos) * 2 + 1 - core, 1)], mine, s_w.at[2], r_k.at[0], dev(pos, 1 - core))

    for v in THREE_FLAT:
        second_hop(v)
    hidden_wait(2, 1)
    for p, (_, col, width) in enumerate(PORTIONS):
        half = hbuf.at[pl.ds(pl.multiple_of(core * 512, 512), 512), pl.ds(col, width)]
        send(half, half, s_x.at[p], r_x.at[p], dev(pos, 1 - core))
    for v in TWO_FLAT:
        second_hop(v)
    for v in ONE:
        axis = ROUTES[v][0]
        deliver(lambda c: w_ref.at[:, columns(chip(shift(v)) * 2 + c, 1)], v, (axis, v[axis]))
    for v in sorted(THREE_FLAT):
        third_hop(v)

    for p, (_, col, width) in enumerate(PORTIONS):
        wait(hbuf.at[pl.ds(0, 512), pl.ds(col, width)], r_x.at[p])

    def product(dz, dy, first):
        wait(wbuf.at[pl.ds(0, 256)], r_k.at[dz * 4 + dy])
        k0 = pl.multiple_of((((pos[Z] - dz) % 4) * 4 + (pos[Y] - dy) % 4) * 256, 256)
        for t in range(4):
            cols = pl.ds(t * 256, 256)
            part = jnp.dot(hbuf[:, pl.ds(k0, 256)], wbuf[pl.ds(k0, 256), cols], preferred_element_type=jnp.float32)
            if first:
                acc[:, cols] = part
            else:
                acc[:, cols] += part

    product(0, 0, True)

    @pl.loop(1, 7)
    def _(i):
        near = i < 4
        product(jnp.where(near, i, 0), jnp.where(near, 0, i - 3), False)

    @pl.loop(0, 9)
    def _(i):
        product(1 + i // 3, 1 + i % 3, False)

    @pl.loop(0, 64)
    def _(i):
        top = acc[pl.ds(pl.multiple_of(i * 8, 8), 8), :]
        low = acc[pl.ds(pl.multiple_of(512 + i * 8, 8), 8), :]
        out_ref[pl.ds(pl.multiple_of(i * 16, 16), 16), :] = jnp.concatenate([top, low], axis=0).astype(jnp.bfloat16)

    wait(st_a, s_w.at[0])
    wait(st_b, s_w.at[1])
    wait(wbuf.at[pl.ds(0, 127 * 32)], s_w.at[2])
    for p, (_, col, width) in enumerate(PORTIONS):
        wait(hbuf.at[pl.ds(0, 63 * 8), pl.ds(col, width)], s_h.at[p])
        wait(hbuf.at[pl.ds(0, 512), pl.ds(col, width)], s_x.at[p])


def solution(mesh):
    def local_part(hid_blk, w_blk):
        dma = pltpu.SemaphoreType.DMA
        return pl.pallas_call(
            _kernel,
            out_shape=jax.ShapeDtypeStruct((1024, 1024), jnp.bfloat16),
            in_specs=[pl.BlockSpec(memory_space=pl.ANY)] * 2,
            out_specs=pl.BlockSpec(memory_space=pltpu.VMEM),
            scratch_shapes=[
                pltpu.VMEM((1024, 4096), jnp.bfloat16),
                pltpu.VMEM((4096, 1024), jnp.bfloat16),
                pltpu.VMEM((len(FIRST), 32, 2048), jnp.bfloat16),
                pltpu.VMEM((len(THREE_FLAT), 32, 2048), jnp.bfloat16),
                pltpu.VMEM((1024, 1024), jnp.float32),
                dma((len(FIRST),)),
                dma((len(THREE_FLAT),)),
                dma((16,)),
                dma((3,)),
                dma((36,)),
                dma((3,)),
                dma((3,)),
                dma((3,)),
                dma,
            ],
            compiler_params=pltpu.CompilerParams(
                collective_id=0, has_side_effects=True, vmem_limit_bytes=58 * 2**20
            ),
        )(hid_blk, w_blk)

    return jax.shard_map(
        local_part,
        mesh=mesh,
        in_specs=(P(("dp", "tp"), None), P(("dp", "tp"), None)),
        out_specs=P(None, ("dp", "tp")),
        check_vma=False,
    )
```

time: 310 us -> 127 us (0.41)
  blocking collectives: 220 us -> 0 us
  Pallas kernels: 0 us -> 122 us
  local copies, waits for them, and re-layouts: 56.6 us -> 3.08 us
  matrix products: 14.6 us -> 0 us
  between operations: 13.4 us -> 0.01 us
    all_to_all x2 -> x0, blocking collectives: 220 us -> none  [the longest x1 114 us: local_part(): w_step = lax.all_to_all(w_split, 'tp', 2, 0, tiled=True)]
    pallas_call x0 -> x1, Pallas kernels: none -> 122 us  [local_part(): pl.pallas_call(_kernel, out_shape=jax.ShapeDtypeStruct((1024, 1024), jnp....]
    all_to_all x3 -> x0, local copies, waits for them, and re-layouts: 33.9 us -> none  [the longest x2 22.6 us: local_part(): w_cols = lax.all_to_all(w_step, 'dp', 1, 0, tiled=True)]
    dot_general x1 -> x0, matrix products: 14.6 us -> none  [local_part(): jnp.dot(full_hidden, w_cols, preferred_element_type=jnp.float32)]
    reshape x1 -> x0, local copies, waits for them, and re-layouts: 11.3 us -> none  [local_part(): w_split = w_blk.reshape(rows_loc, outer_size, inner_size, col_width)]
    unnamed x1, local copies, waits for them, and re-layouts: 11.4 us -> 3.08 us
  transfers between devices with their start and end apart: 1 -> 0, of which waited for: 0 -> 0; matrix products, arithmetic and copies ran while one was open for 19% -> 0% of each run, Pallas kernels for 0% -> 0%
where the time goes in v1:
time: 127 us; the launch traced here: 125 us
  Pallas kernels  122 us (96%)
  local copies, waits for them, and re-layouts  3.08 us (2%)
    pallas_call x1, Pallas kernels, local_part(): pl.pallas_call(_kernel, out_shape=jax.ShapeDtypeStruct((1024, 1024), jnp....  122 us
    unnamed x1, local copies, waits for them, and re-layouts  3.08 us

profile of v1, /device:TPU:1, one launch (start us, length us, event | category | flops | bytes accessed | tf_op | source)
XLA Modules:
  0.0 125.2 jit_solution(7497840276029108765)
XLA Ops:
  0.0 122.1 %shard_map.28 = bf16[1024,1024]{1,0:T(8,128)(2,1)} custom-call(bf16[8,4096]{1,0:T(8,128)(2,1)} %hid_ref.1, bf16[32,131072]{1,0:T(8,128)(2,1)} %w_ref.1), custom_call_target="tpu_custom_call" | custom-call | tf_op jit(solution)/shard_map/pallas_call | solution.py:267
  122.1 3.1 %copy.4 = bf16[1024,1024]{1,0:T(8,128)(2,1)} copy(bf16[1024,1024]{1,0:T(8,128)(2,1)} %shard_map.28) | data formatting | bytes 4194304

commit v2 on v1

--- a/solution.py
+++ b/solution.py
@@ -24,7 +24,7 @@
     for v in [(a, b, c) for a in range(4) for b in range(4) for c in range(4)]:
         if v == (0, 0, 0):
             continue
-        w, order = v, (Z, Y, X)
+        w, order = v, tuple(sorted((Z, Y, X), key=lambda a: v[a] != 2))
         for _ in range(3):
             for u in (w, _neg(w)):
                 if u not in routes:
@@ -57,7 +57,16 @@
 THREE_FLAT = [v for g in THREE for v in g]
 TWO_FLAT = [v for g in TWO for v in g]
 FIRST = THREE_FLAT + TWO_FLAT
-PORTIONS = (((X, Y, Z), 0, 1408), ((Y, Z, X), 1408, 1408), ((Z, X, Y), 2816, 1280))
+GROUPS = {g[0]: g for g in THREE + TWO}
+BATCHES = (
+    GROUPS[1, 1, 2] + GROUPS[1, 1, 1] + GROUPS[2, 2, 2],
+    GROUPS[1, 2, 2],
+    GROUPS[1, 2, 3],
+    GROUPS[1, 1, 3] + GROUPS[0, 1, 1],
+    GROUPS[0, 1, 2],
+    GROUPS[0, 1, 3] + GROUPS[0, 2, 1] + GROUPS[0, 2, 2],
+)
+PORTIONS = (((X, Y, Z), 0, 1152), ((Y, Z, X), 1152, 1536), ((Z, X, Y), 2688, 1408))
 
 
 def _kernel(hid_ref, w_ref, out_ref, hbuf, wbuf, st_a, st_b, acc, r_a, r_b, r_k, s_w, r_h, s_h, r_x, s_x, l_sem):
@@ -163,7 +172,7 @@
         to = shift(unit(axis, d))
         origin = tuple((t - o) % 4 for t, o in zip(to, v))
         at = wbuf.at[pl.ds(pl.multiple_of((chip(origin) * 2 + core) * 32, 32), 32)]
-        for c in range(2):
+        for c in (1, 0) if sum(v) % 2 else (0, 1):
             send(src_of(c), at, s_w.at[2], r_k.at[v[Z] * 4 + v[Y]], dev(to, c))
 
     def second_hop(v):
@@ -188,24 +197,19 @@
     pltpu.make_async_copy(hid_ref, slot, l_sem).start()
     pltpu.make_async_copy(w_ref.at[:, columns(me, 1)], mine, r_k.at[0]).start()
 
-    fill = [[v for v in g] for g in THREE]
-    batches = [fill[0], fill[1], fill[2], fill[3], [v for g in fill[4:] for v in g]]
-    n = 0
-    for phase in range(3):
-        for step in range(2):
-            hidden_send(phase, step)
-            if n < len(batches):
-                for v in batches[n]:
-                    first_hop(v)
-            n += 1
-            if phase == 0 and step == 0:
-                wait(slot, l_sem)
-            if phase == 2:
-                for g in TWO[:2] if step == 0 else TWO[2:]:
-                    for v in g:
-                        first_hop(v)
-            if (phase, step) != (2, 1):
-                hidden_wait(phase, step)
+    for n, batch in enumerate(BATCHES):
+        phase, step = divmod(n, 2)
+        hidden_send(phase, step)
+        if n == 1:
+            for v in ONE:
+                axis = ROUTES[v][0]
+                deliver(lambda c: w_ref.at[:, columns(chip(shift(v)) * 2 + c, 1)], v, (axis, v[axis]))
+        for v in batch:
+            first_hop(v)
+        if n == 0:
+            wait(slot, l_sem)
+        if n < 5:
+            hidden_wait(phase, step)
     send(w_ref.at[:, columns(chip(pos) * 2 + 1 - core, 1)], mine, s_w.at[2], r_k.at[0], dev(pos, 1 - core))
 
     for v in THREE_FLAT:
@@ -216,9 +220,6 @@
         send(half, half, s_x.at[p], r_x.at[p], dev(pos, 1 - core))
     for v in TWO_FLAT:
         second_hop(v)
-    for v in ONE:
-        axis = ROUTES[v][0]
-        deliver(lambda c: w_ref.at[:, columns(chip(shift(v)) * 2 + c, 1)], v, (axis, v[axis]))
     for v in sorted(THREE_FLAT):
         third_hop(v)
 
@@ -266,7 +267,7 @@
         dma = pltpu.SemaphoreType.DMA
         return pl.pallas_call(
             _kernel,
-            out_shape=jax.ShapeDtypeStruct((1024, 1024), jnp.bfloat16),
+            out_shape=pltpu.VMEM((1024, 1024), jnp.bfloat16),
             in_specs=[pl.BlockSpec(memory_space=pl.ANY)] * 2,
             out_specs=pl.BlockSpec(memory_space=pltpu.VMEM),
             scratch_shapes=[

time: 127 us -> 121 us (0.953); the launches traced: 125 us -> 121 us
  Pallas kernels: 122 us -> 119 us
  local copies, waits for them, and re-layouts: 3.08 us -> 1.32 us
    pallas_call x1, Pallas kernels: 122 us -> 119 us  [local_part(): pl.pallas_call(_kernel, out_shape=pltpu.VMEM((1024, 1024), jnp.bfloat16),...]
    unnamed x1, local copies, waits for them, and re-layouts: 3.08 us -> 1.32 us
where the time goes in v2:
time: 121 us
  Pallas kernels  119 us (98%)
  local copies, waits for them, and re-layouts  1.32 us (1%)
    pallas_call x1, Pallas kernels, local_part(): pl.pallas_call(_kernel, out_shape=pltpu.VMEM((1024, 1024), jnp.bfloat16),...  119 us

profile of v2, /device:TPU:1, one launch (start us, length us, event | category | flops | bytes accessed | tf_op | source)
XLA Modules:
  0.0 120.5 jit_solution(7937743898867884769)
XLA Ops:
  0.0 119.2 %shard_map.28 = bf16[1024,1024]{1,0:T(8,128)(2,1)S(1)} custom-call(bf16[8,4096]{1,0:T(8,128)(2,1)} %hid_ref.1, bf16[32,131072]{1,0:T(8,128)(2,1)} %w_ref.1), custom_call_target="tpu_custom_call" | custom-call | tf_op jit(solution)/shard_map/pallas_call | solution.py:268
  119.2 1.3 %copy.4 = bf16[1024,1024]{1,0:T(8,128)(2,1)} copy(bf16[1024,1024]{1,0:T(8,128)(2,1)S(1)} %shard_map.28) | data formatting | bytes 4194304

commit v3 on v2

--- a/solution.py
+++ b/solution.py
@@ -19,57 +19,79 @@
     return tuple(-t % 4 for t in v)
 
 
-def _routes():
-    routes = {}
-    for v in [(a, b, c) for a in range(4) for b in range(4) for c in range(4)]:
-        if v == (0, 0, 0):
-            continue
-        w, order = v, tuple(sorted((Z, Y, X), key=lambda a: v[a] != 2))
-        for _ in range(3):
-            for u in (w, _neg(w)):
-                if u not in routes:
-                    routes[u] = tuple(a for a in order if u[a])
-            w, order = _turn(w), tuple((a + 1) % 3 for a in order)
-    routes[(1, 1, 1)], routes[(2, 2, 2)], routes[(3, 3, 3)] = (Z, Y, X), (Y, X, Z), (X, Z, Y)
-    return routes
-
-
-def _orbits(offsets):
-    seen, groups = set(), []
-    for v in offsets:
-        if v in seen:
-            continue
-        group, w = [], v
-        for _ in range(3):
-            for u in (w, _neg(w)):
-                if u not in seen:
-                    seen.add(u)
-                    group.append(u)
-            w = _turn(w)
-        groups.append(group)
-    return groups
-
-
-ROUTES = _routes()
-THREE = _orbits([v for v in ROUTES if len(ROUTES[v]) == 3])
-TWO = _orbits([v for v in ROUTES if len(ROUTES[v]) == 2])
-ONE = [v for v in ROUTES if len(ROUTES[v]) == 1]
-THREE_FLAT = [v for g in THREE for v in g]
-TWO_FLAT = [v for g in TWO for v in g]
+def _last(v):
+    z, y, x = v
+    if sum(map(bool, v)) == 1:
+        return next(a for a in range(3) if v[a])
+    if x == 0:
+        return Y if z == 2 or (y != 2 and z != y) else Z
+    if z == 0 or y == 0:
+        line, axis = (y, Y) if z == 0 else (z, Z)
+        return axis if line != 2 and x in (2, line) else X
+    if z == 2 and y == 2:
+        return Y if x == 2 else X
+    if z == 2:
+        return Y if x in (2, y) else X
+    if y == 2:
+        return Z if x in (2, z) else X
+    return Z if x == 2 else Y if x == z else X
+
+
+def _route(v):
+    last = _last(v)
+    rest = [a for a in range(3) if v[a] and a != last]
+    if len(rest) == 2:
+        longer = [a for a in rest if v[a] == 2]
+        if len(longer) == 1:
+            first = longer[0]
+        elif longer:
+            first = X if X in rest else Z if v[X] == 1 else Y
+        else:
+            first = Z if last == Y else Y
+        rest = [first] + [a for a in rest if a != first]
+    return (*rest, last)
+
+
+ALL = [(a, b, c) for a in range(4) for b in range(4) for c in range(4)][1:]
+ROUTES = {v: _route(v) for v in ALL}
+ONE = [v for v in ALL if len(ROUTES[v]) == 1]
+
+
+def _lines(*lines):
+    return [(*line, x) for line in lines for x in (1, 2, 3)]
+
+
+G = dict(
+    Q=_lines((2, 1), (2, 3), (1, 2), (3, 2)),
+    T=_lines((2, 2)),
+    P=_lines((1, 3), (3, 1)),
+    R=_lines((1, 1), (3, 3)),
+    A=_lines((0, 1), (0, 3)),
+    B=_lines((0, 2)),
+    C=_lines((2, 0)),
+    D=_lines((1, 0), (3, 0)),
+    E=[(a, b, 0) for a, b in ((2, 2), (2, 1), (2, 3), (1, 2), (3, 2), (1, 3), (3, 1), (1, 1), (3, 3))],
+)
+G["O"] = ONE
+THREE_FLAT = G["T"] + G["Q"] + G["P"] + G["R"]
+TWO_FLAT = G["A"] + G["D"] + G["B"] + G["C"] + G["E"]
 FIRST = THREE_FLAT + TWO_FLAT
-GROUPS = {g[0]: g for g in THREE + TWO}
+
+
+ORDER = [(0, 0), (0, 1), (0, 3), (1, 0), (3, 0), (0, 2), (2, 0), (2, 2), (1, 2), (3, 2), (2, 1), (2, 3), (1, 3), (3, 1), (1, 1), (3, 3)]
 BATCHES = (
-    GROUPS[1, 1, 2] + GROUPS[1, 1, 1] + GROUPS[2, 2, 2],
-    GROUPS[1, 2, 2],
-    GROUPS[1, 2, 3],
-    GROUPS[1, 1, 3] + GROUPS[0, 1, 1],
-    GROUPS[0, 1, 2],
-    GROUPS[0, 1, 3] + GROUPS[0, 2, 1] + GROUPS[0, 2, 2],
+    G["Q"],
+    G["O"] + G["T"],
+    G["P"] + G["R"],
+    G["A"] + G["B"] + G["C"],
+    G["D"] + G["E"],
+    [],
 )
+LATE = 2
 PORTIONS = (((X, Y, Z), 0, 1152), ((Y, Z, X), 1152, 1536), ((Z, X, Y), 2688, 1408))
 
 
-def _kernel(hid_ref, w_ref, out_ref, hbuf, wbuf, st_a, st_b, acc, r_a, r_b, r_k, s_w, r_h, s_h, r_x, s_x, l_sem):
+def _kernel(hid_ref, w_ref, acc, hbuf, wbuf, st_a, st_b, r_a, r_b, r_k, s_w, r_h, s_h, r_x, s_x, l_sem):
     dp, tp = lax.axis_index("dp"), lax.axis_index("tp")
     pos, core = (dp // 4, dp % 4, tp // 2), tp % 2
 
@@ -172,7 +194,7 @@
         to = shift(unit(axis, d))
         origin = tuple((t - o) % 4 for t, o in zip(to, v))
         at = wbuf.at[pl.ds(pl.multiple_of((chip(origin) * 2 + core) * 32, 32), 32)]
-        for c in (1, 0) if sum(v) % 2 else (0, 1):
+        for c in (0, 1) if v[Z] == 1 or (v[Z] in (0, 2) and v[Y] == 1) else (1, 0):
             send(src_of(c), at, s_w.at[2], r_k.at[v[Z] * 4 + v[Y]], dev(to, c))
 
     def second_hop(v):
@@ -191,6 +213,10 @@
         axis = ROUTES[v][2]
         deliver(lambda c: st_b.at[j, :, pl.ds(c * 1024, 1024)], v, (axis, v[axis]))
 
+    def single_hop(v):
+        axis = ROUTES[v][0]
+        deliver(lambda c: w_ref.at[:, columns(chip(shift(v)) * 2 + c, 1)], v, (axis, v[axis]))
+
     me = chip(pos) * 2 + core
     mine = wbuf.at[pl.ds(pl.multiple_of(me * 32, 32), 32)]
     slot = hbuf.at[rows(core * 64 + chip(pos))]
@@ -200,12 +226,11 @@
     for n, batch in enumerate(BATCHES):
         phase, step = divmod(n, 2)
         hidden_send(phase, step)
-        if n == 1:
-            for v in ONE:
-                axis = ROUTES[v][0]
-                deliver(lambda c: w_ref.at[:, columns(chip(shift(v)) * 2 + c, 1)], v, (axis, v[axis]))
         for v in batch:
-            first_hop(v)
+            if len(ROUTES[v]) == 1:
+                single_hop(v)
+            else:
+                first_hop(v)
         if n == 0:
             wait(slot, l_sem)
         if n < 5:
@@ -214,13 +239,13 @@
 
     for v in THREE_FLAT:
         second_hop(v)
+    for v in TWO_FLAT:
+        second_hop(v)
     hidden_wait(2, 1)
     for p, (_, col, width) in enumerate(PORTIONS):
         half = hbuf.at[pl.ds(pl.multiple_of(core * 512, 512), 512), pl.ds(col, width)]
         send(half, half, s_x.at[p], r_x.at[p], dev(pos, 1 - core))
-    for v in TWO_FLAT:
-        second_hop(v)
-    for v in sorted(THREE_FLAT):
+    for v in THREE_FLAT:
         third_hop(v)
 
     for p, (_, col, width) in enumerate(PORTIONS):
@@ -237,22 +262,10 @@
             else:
                 acc[:, cols] += part
 
-    product(0, 0, True)
-
-    @pl.loop(1, 7)
-    def _(i):
-        near = i < 4
-        product(jnp.where(near, i, 0), jnp.where(near, 0, i - 3), False)
-
-    @pl.loop(0, 9)
-    def _(i):
-        product(1 + i // 3, 1 + i % 3, False)
-
-    @pl.loop(0, 64)
-    def _(i):
-        top = acc[pl.ds(pl.multiple_of(i * 8, 8), 8), :]
-        low = acc[pl.ds(pl.multiple_of(512 + i * 8, 8), 8), :]
-        out_ref[pl.ds(pl.multiple_of(i * 16, 16), 16), :] = jnp.concatenate([top, low], axis=0).astype(jnp.bfloat16)
+    for n, line in enumerate(ORDER[: 16 - LATE]):
+        product(*_mirror(line, core), n == 0)
+    for dz, dy in [_mirror(line, core) for line in ORDER[16 - LATE :]]:
+        wait(wbuf.at[pl.ds(0, 256)], r_k.at[dz * 4 + dy])
 
     wait(st_a, s_w.at[0])
     wait(st_b, s_w.at[1])
@@ -262,34 +275,58 @@
         wait(hbuf.at[pl.ds(0, 512), pl.ds(col, width)], s_x.at[p])
 
 
+def _mirror(line, core):
+    return tuple(d if d in (0, 2) else d + core * (4 - 2 * d) for d in line)
+
+
+def _finish(acc, hbuf, wbuf, out_ref, stage, sem):
+    dp = lax.axis_index("dp")
+    z, y = dp // 4, dp % 4
+    core = lax.axis_index('tp') % 2
+    lines = [_mirror(t, core) for t in ORDER[16 - LATE :]]
+    starts = [pl.multiple_of((((z - dz) % 4) * 4 + (y - dy) % 4) * 256, 256) for dz, dy in lines]
+    W = 256
+
+    def step(t):
+        cols = pl.ds(t * W, W)
+        val = acc[:, cols]
+        for k0 in starts:
+            val += jnp.dot(hbuf[:, pl.ds(k0, 256)], wbuf[pl.ds(k0, 256), cols], preferred_element_type=jnp.float32)
+        for i in range(64):
+            pair = jnp.concatenate([val[i * 8 : i * 8 + 8], val[512 + i * 8 : 512 + i * 8 + 8]], axis=0)
+            stage[i * 16 : i * 16 + 16, cols] = pair.astype(jnp.bfloat16)
+        pltpu.make_async_copy(stage.at[:, cols], out_ref.at[:, cols], sem).start()
+
+    for t in range(1024 // W):
+        step(t)
+    pltpu.make_async_copy(stage, out_ref, sem).wait()
+
+
 def solution(mesh):
     def local_part(hid_blk, w_blk):
         dma = pltpu.SemaphoreType.DMA
-        return pl.pallas_call(
+        vm = pl.BlockSpec(memory_space=pltpu.VMEM)
+        acc, hbuf, wbuf = pl.pallas_call(
             _kernel,
-            out_shape=pltpu.VMEM((1024, 1024), jnp.bfloat16),
+            out_shape=[pltpu.VMEM((1024, 1024), jnp.float32), pltpu.VMEM((1024, 4096), jnp.bfloat16), pltpu.VMEM((4096, 1024), jnp.bfloat16)],
             in_specs=[pl.BlockSpec(memory_space=pl.ANY)] * 2,
-            out_specs=pl.BlockSpec(memory_space=pltpu.VMEM),
+            out_specs=[vm] * 3,
             scratch_shapes=[
-                pltpu.VMEM((1024, 4096), jnp.bfloat16),
-                pltpu.VMEM((4096, 1024), jnp.bfloat16),
                 pltpu.VMEM((len(FIRST), 32, 2048), jnp.bfloat16),
                 pltpu.VMEM((len(THREE_FLAT), 32, 2048), jnp.bfloat16),
-                pltpu.VMEM((1024, 1024), jnp.float32),
-                dma((len(FIRST),)),
-                dma((len(THREE_FLAT),)),
-                dma((16,)),
-                dma((3,)),
-                dma((36,)),
-                dma((3,)),
-                dma((3,)),
-                dma((3,)),
-                dma,
+                dma((len(FIRST),)), dma((len(THREE_FLAT),)), dma((16,)), dma((3,)), dma((36,)), dma((3,)), dma((3,)), dma((3,)), dma,
             ],
-            compiler_params=pltpu.CompilerParams(
-                collective_id=0, has_side_effects=True, vmem_limit_bytes=58 * 2**20
-            ),
+            compiler_params=pltpu.CompilerParams(collective_id=0, has_side_effects=True, vmem_limit_bytes=38 * 2**20),
         )(hid_blk, w_blk)
+        acc, hbuf, wbuf = (pltpu.with_memory_space_constraint(t, pltpu.VMEM) for t in (acc, hbuf, wbuf))
+        return pl.pallas_call(
+            _finish,
+            out_shape=jax.ShapeDtypeStruct((1024, 1024), jnp.bfloat16),
+            in_specs=[vm] * 3,
+            out_specs=pl.BlockSpec(memory_space=pl.ANY),
+            scratch_shapes=[pltpu.VMEM((1024, 1024), jnp.bfloat16), dma],
+            compiler_params=pltpu.CompilerParams(vmem_limit_bytes=20 * 2**20),
+        )(acc, hbuf, wbuf)
 
     return jax.shard_map(
         local_part,

time: 121 us -> 118 us (0.975)
  local copies, waits for them, and re-layouts: 1.32 us -> 0 us
    unnamed x1 -> x0, local copies, waits for them, and re-layouts: 1.32 us -> none
    pallas_call x1 -> x2, Pallas kernels: 119 us -> 118 us  [the longest x1 116 us: local_part(): pl.pallas_call(_kernel, out_shape=[pltpu.VMEM((1024, 1024), jnp.float32),...]
where the time goes in v3:
time: 118 us
  Pallas kernels  118 us (100%)
    pallas_call x1, Pallas kernels, local_part(): pl.pallas_call(_kernel, out_shape=[pltpu.VMEM((1024, 1024), jnp.float32),...  116 us

profile of v3, /device:TPU:1, one launch (start us, length us, event | category | flops | bytes accessed | tf_op | source)
XLA Modules:
  0.0 118.3 jit_solution(780160509926824807)
XLA Ops:
  0.0 115.9 %shard_map.28 = (f32[1024,1024]{1,0:T(8,128)S(1)}, bf16[1024,4096]{1,0:T(8,128)(2,1)S(1)}, bf16[4096,1024]{1,0:T(8,128)(2,1)S(1)}) custom-call(bf16[8,4096]{1,0:T(8,128)(2,1)} %hid_ref.1, bf16[32,131072]{1,0:T(8,128)(2,1)} %w_ref.1), custom_call_target="tpu_custom_call" | custom-call | tf_op jit(solution)/shard_map/pallas_call | solution.py:309
  115.9 2.4 %shard_map.29 = bf16[1024,1024]{1,0:T(8,128)(2,1)} custom-call(f32[1024,1024]{1,0:T(8,128)S(1)} %get-tuple-element.8.acc, bf16[1024,4096]{1,0:T(8,128)(2,1)S(1)} %get-tuple-element.9.hbuf, bf16[4096,1024]{1,0:T(8,128)(2,1)S(1)} %get-tuple-element.10.wbuf), custom_call_target="tpu_custom_call" | custom-call | tf_op jit(solution)/shard_map/pallas_call | solution.py:322

commit v4 on v3

--- a/solution.py
+++ b/solution.py
@@ -75,20 +75,23 @@
 G["O"] = ONE
 THREE_FLAT = G["T"] + G["Q"] + G["P"] + G["R"]
 TWO_FLAT = G["A"] + G["D"] + G["B"] + G["C"] + G["E"]
+GROUP = {v: n for n, g in enumerate('TQPRADBCE') for v in G[g]}
 FIRST = THREE_FLAT + TWO_FLAT
 
 
 ORDER = [(0, 0), (0, 1), (0, 3), (1, 0), (3, 0), (0, 2), (2, 0), (2, 2), (1, 2), (3, 2), (2, 1), (2, 3), (1, 3), (3, 1), (1, 1), (3, 3)]
-BATCHES = (
-    G["Q"],
-    G["O"] + G["T"],
-    G["P"] + G["R"],
-    G["A"] + G["B"] + G["C"],
-    G["D"] + G["E"],
-    [],
+LATE = 1
+SCHEDULE = (
+    "H0", "1Q", "SS", "W0",
+    "H1", "1O", "1T", "W1",
+    "H2", "1P", "1R", "W2",
+    "H3", "1A", "1B", "1C", "1D", "W3",
+    "H4", "1E", "2T", "2Q", "W4",
+    "H5", "CC", "2P", "2R", "2A", "2D", "2B", "2C",
+    "2E", "3T", "3Q", "W5",
+    "XX", "3P", "3R",
 )
-LATE = 2
-PORTIONS = (((X, Y, Z), 0, 1152), ((Y, Z, X), 1152, 1536), ((Z, X, Y), 2688, 1408))
+PORTIONS = (((X, Y, Z), 0, 1280), ((Y, Z, X), 1280, 1408), ((Z, X, Y), 2688, 1408))
 
 
 def _kernel(hid_ref, w_ref, acc, hbuf, wbuf, st_a, st_b, r_a, r_b, r_k, s_w, r_h, s_h, r_x, s_x, l_sem):
@@ -150,9 +153,6 @@
             return [(s, n // 2, col, width)], [(s + n // 2, n // 2, col, width)]
         m = len(part) // 2
         return [(s, n, col, width) for s, n in part[:m]], [(s, n, col, width) for s, n in part[m:]]
-
-    def sem_h(p, phase, step, side):
-        return r_h.at[((p * 3 + phase) * 2 + step) * 2 + side]
 
     def hidden_send(phase, step):
         for p, (order, col, width) in enumerate(PORTIONS):
@@ -166,20 +166,11 @@
                 for s, n, c0, cw in items:
                     dst = hbuf.at[rows(s, n), pl.ds(c0, cw)]
                     src = hid_ref.at[:, pl.ds(c0, cw)] if phase == 0 and step == 0 else dst
-                    send(src, dst, s_h.at[p], sem_h(p, phase, step, side), to)
+                    send(src, dst, s_h, r_h.at[phase * 2 + step], to)
 
     def hidden_wait(phase, step):
-        for p, (order, col, width) in enumerate(PORTIONS):
-            n = 4**phase
-            for side in range(2):
-                if step == 0:
-                    ref = hbuf.at[pl.ds(0, n * 8), pl.ds(col, width)]
-                elif phase == 0:
-                    cut = (width // 2 + 127) // 128 * 128
-                    ref = hbuf.at[pl.ds(0, 8), pl.ds(col, cut if side == 0 else width - cut)]
-                else:
-                    ref = hbuf.at[pl.ds(0, n * 4), pl.ds(col, width)]
-                wait(ref, sem_h(p, phase, step, side))
+        n = 4**phase * (2, 1)[step]
+        wait(hbuf.at[pl.ds(0, n * 8)], r_h.at[phase * 2 + step])
 
     def columns(c, n):
         return pl.ds(pl.multiple_of(c * 1024, 1024), n * 1024)
@@ -187,7 +178,7 @@
     def first_hop(v):
         i = FIRST.index(v)
         to = shift(unit(ROUTES[v][0], v[ROUTES[v][0]]))
-        send(w_ref.at[:, columns(chip(shift(v)) * 2, 2)], st_a.at[i], s_w.at[0], r_a.at[i], dev(to, core))
+        send(w_ref.at[:, columns(chip(shift(v)) * 2, 2)], st_a.at[i], s_w.at[0], r_a.at[GROUP[v]], dev(to, core))
 
     def deliver(src_of, v, last):
         axis, d = last
@@ -199,17 +190,15 @@
 
     def second_hop(v):
         i = FIRST.index(v)
-        wait(st_a.at[i], r_a.at[i])
         axis = ROUTES[v][1]
         if len(ROUTES[v]) == 2:
             deliver(lambda c: st_a.at[i, :, pl.ds(c * 1024, 1024)], v, (axis, v[axis]))
         else:
             j = THREE_FLAT.index(v)
-            send(st_a.at[i], st_b.at[j], s_w.at[1], r_b.at[j], dev(shift(unit(axis, v[axis])), core))
+            send(st_a.at[i], st_b.at[j], s_w.at[1], r_b.at[GROUP[v]], dev(shift(unit(axis, v[axis])), core))
 
     def third_hop(v):
         j = THREE_FLAT.index(v)
-        wait(st_b.at[j], r_b.at[j])
         axis = ROUTES[v][2]
         deliver(lambda c: st_b.at[j, :, pl.ds(c * 1024, 1024)], v, (axis, v[axis]))
 
@@ -223,33 +212,34 @@
     pltpu.make_async_copy(hid_ref, slot, l_sem).start()
     pltpu.make_async_copy(w_ref.at[:, columns(me, 1)], mine, r_k.at[0]).start()
 
-    for n, batch in enumerate(BATCHES):
-        phase, step = divmod(n, 2)
-        hidden_send(phase, step)
-        for v in batch:
-            if len(ROUTES[v]) == 1:
-                single_hop(v)
-            else:
-                first_hop(v)
-        if n == 0:
+    for kind, which in SCHEDULE:
+        if kind == "H":
+            hidden_send(*divmod(int(which), 2))
+        elif kind == "W":
+            hidden_wait(*divmod(int(which), 2))
+        elif kind == "S":
             wait(slot, l_sem)
-        if n < 5:
-            hidden_wait(phase, step)
-    send(w_ref.at[:, columns(chip(pos) * 2 + 1 - core, 1)], mine, s_w.at[2], r_k.at[0], dev(pos, 1 - core))
-
-    for v in THREE_FLAT:
-        second_hop(v)
-    for v in TWO_FLAT:
-        second_hop(v)
-    hidden_wait(2, 1)
-    for p, (_, col, width) in enumerate(PORTIONS):
-        half = hbuf.at[pl.ds(pl.multiple_of(core * 512, 512), 512), pl.ds(col, width)]
-        send(half, half, s_x.at[p], r_x.at[p], dev(pos, 1 - core))
-    for v in THREE_FLAT:
-        third_hop(v)
-
-    for p, (_, col, width) in enumerate(PORTIONS):
-        wait(hbuf.at[pl.ds(0, 512), pl.ds(col, width)], r_x.at[p])
+        elif kind == "1":
+            for v in G[which]:
+                if len(ROUTES[v]) == 1:
+                    single_hop(v)
+                else:
+                    first_hop(v)
+        elif kind == "2":
+            wait(st_a.at[pl.ds(FIRST.index(G[which][0]), len(G[which]))], r_a.at[GROUP[G[which][0]]])
+            for v in G[which]:
+                second_hop(v)
+        elif kind == "3":
+            wait(st_b.at[pl.ds(FIRST.index(G[which][0]), len(G[which]))], r_b.at[GROUP[G[which][0]]])
+            for v in G[which]:
+                third_hop(v)
+        elif kind == "C":
+            send(w_ref.at[:, columns(chip(pos) * 2 + 1 - core, 1)], mine, s_w.at[2], r_k.at[0], dev(pos, 1 - core))
+        else:
+            half = hbuf.at[pl.ds(pl.multiple_of(core * 512, 512), 512)]
+            send(half, half, s_x, r_x, dev(pos, 1 - core))
+
+    wait(hbuf.at[pl.ds(0, 512)], r_x)
 
     def product(dz, dy, first):
         wait(wbuf.at[pl.ds(0, 256)], r_k.at[dz * 4 + dy])
@@ -270,9 +260,8 @@
     wait(st_a, s_w.at[0])
     wait(st_b, s_w.at[1])
     wait(wbuf.at[pl.ds(0, 127 * 32)], s_w.at[2])
-    for p, (_, col, width) in enumerate(PORTIONS):
-        wait(hbuf.at[pl.ds(0, 63 * 8), pl.ds(col, width)], s_h.at[p])
-        wait(hbuf.at[pl.ds(0, 512), pl.ds(col, width)], s_x.at[p])
+    wait(hbuf.at[pl.ds(0, 63 * 8)], s_h)
+    wait(hbuf.at[pl.ds(0, 512)], s_x)
 
 
 def _mirror(line, core):
@@ -314,7 +303,7 @@
             scratch_shapes=[
                 pltpu.VMEM((len(FIRST), 32, 2048), jnp.bfloat16),
                 pltpu.VMEM((len(THREE_FLAT), 32, 2048), jnp.bfloat16),
-                dma((len(FIRST),)), dma((len(THREE_FLAT),)), dma((16,)), dma((3,)), dma((36,)), dma((3,)), dma((3,)), dma((3,)), dma,
+                dma((9,)), dma((4,)), dma((16,)), dma((3,)), dma((6,)), dma, dma, dma, dma,
             ],
             compiler_params=pltpu.CompilerParams(collective_id=0, has_side_effects=True, vmem_limit_bytes=38 * 2**20),
         )(hid_blk, w_blk)

time: 118 us -> 117 us (level)
    pallas_call x1, Pallas kernels: 116 us -> 115 us  [local_part(): pl.pallas_call(_kernel, out_shape=[pltpu.VMEM((1024, 1024), jnp.float32),...]
where the time goes in v4:
time: 117 us
  Pallas kernels  117 us (100%)
    pallas_call x1, Pallas kernels, local_part(): pl.pallas_call(_kernel, out_shape=[pltpu.VMEM((1024, 1024), jnp.float32),...  115 us

profile of v4, /device:TPU:1, one launch (start us, length us, event | category | flops | bytes accessed | tf_op | source)
XLA Modules:
  0.0 116.6 jit_solution(18378726135058745245)
XLA Ops:
  0.0 114.7 %shard_map.28 = (f32[1024,1024]{1,0:T(8,128)S(1)}, bf16[1024,4096]{1,0:T(8,128)(2,1)S(1)}, bf16[4096,1024]{1,0:T(8,128)(2,1)S(1)}) custom-call(bf16[8,4096]{1,0:T(8,128)(2,1)} %hid_ref.1, bf16[32,131072]{1,0:T(8,128)(2,1)} %w_ref.1), custom_call_target="tpu_custom_call" | custom-call | tf_op jit(solution)/shard_map/pallas_call | solution.py:298
  114.8 1.8 %shard_map.29 = bf16[1024,1024]{1,0:T(8,128)(2,1)} custom-call(f32[1024,1024]{1,0:T(8,128)S(1)} %get-tuple-element.8.acc, bf16[1024,4096]{1,0:T(8,128)(2,1)S(1)} %get-tuple-element.9.hbuf, bf16[4096,1024]{1,0:T(8,128)(2,1)S(1)} %get-tuple-element.10.wbuf), custom_call_target="tpu_custom_call" | custom-call | tf_op jit(solution)/shard_map/pallas_call | solution.py:311

commit v5 on v4

--- a/solution.py
+++ b/solution.py
@@ -91,7 +91,7 @@
     "2E", "3T", "3Q", "W5",
     "XX", "3P", "3R",
 )
-PORTIONS = (((X, Y, Z), 0, 1280), ((Y, Z, X), 1280, 1408), ((Z, X, Y), 2688, 1408))
+PORTIONS = (((X, Y, Z), 0, 1408), ((Y, Z, X), 1408, 1408), ((Z, X, Y), 2816, 1280))
 
 
 def _kernel(hid_ref, w_ref, acc, hbuf, wbuf, st_a, st_b, r_a, r_b, r_k, s_w, r_h, s_h, r_x, s_x, l_sem):
@@ -274,7 +274,7 @@
     core = lax.axis_index('tp') % 2
     lines = [_mirror(t, core) for t in ORDER[16 - LATE :]]
     starts = [pl.multiple_of((((z - dz) % 4) * 4 + (y - dy) % 4) * 256, 256) for dz, dy in lines]
-    W = 256
+    W = 512
 
     def step(t):
         cols = pl.ds(t * W, W)

time: 117 us -> 116 us (level)
  no operation moved by 1% of the time
where the time goes in v5:
time: 116 us
  Pallas kernels  116 us (100%)
    pallas_call x1, Pallas kernels, local_part(): pl.pallas_call(_kernel, out_shape=[pltpu.VMEM((1024, 1024), jnp.float32),...  115 us

profile of v5, /device:TPU:1, one launch (start us, length us, event | category | flops | bytes accessed | tf_op | source)
XLA Modules:
  0.0 116.3 jit_solution(10967390692395109409)
XLA Ops:
  0.0 114.5 %shard_map.28 = (f32[1024,1024]{1,0:T(8,128)S(1)}, bf16[1024,4096]{1,0:T(8,128)(2,1)S(1)}, bf16[4096,1024]{1,0:T(8,128)(2,1)S(1)}) custom-call(bf16[8,4096]{1,0:T(8,128)(2,1)} %hid_ref.1, bf16[32,131072]{1,0:T(8,128)(2,1)} %w_ref.1), custom_call_target="tpu_custom_call" | custom-call | tf_op jit(solution)/shard_map/pallas_call | solution.py:298
  114.5 1.8 %shard_map.29 = bf16[1024,1024]{1,0:T(8,128)(2,1)} custom-call(f32[1024,1024]{1,0:T(8,128)S(1)} %get-tuple-element.8.acc, bf16[1024,4096]{1,0:T(8,128)(2,1)S(1)} %get-tuple-element.9.hbuf, bf16[4096,1024]{1,0:T(8,128)(2,1)S(1)} %get-tuple-element.10.wbuf), custom_call_target="tpu_custom_call" | custom-call | tf_op jit(solution)/shard_map/pallas_call | solution.py:311

commit v6 on v5

--- a/solution.py
+++ b/solution.py
@@ -75,7 +75,10 @@
 G["O"] = ONE
 THREE_FLAT = G["T"] + G["Q"] + G["P"] + G["R"]
 TWO_FLAT = G["A"] + G["D"] + G["B"] + G["C"] + G["E"]
-GROUP = {v: n for n, g in enumerate('TQPRADBCE') for v in G[g]}
+G["V"] = G["P"] + G["R"]
+G["F"] = G["A"] + G["D"] + G["B"] + G["C"]
+GROUP = {v: n for n, g in enumerate("TQVFE") for v in G[g]}
+GROUP_B = {v: n for n, g in enumerate("TQPR") for v in G[g]}
 FIRST = THREE_FLAT + TWO_FLAT
 
 
@@ -87,14 +90,13 @@
     "H2", "1P", "1R", "W2",
     "H3", "1A", "1B", "1C", "1D", "W3",
     "H4", "1E", "2T", "2Q", "W4",
-    "H5", "CC", "2P", "2R", "2A", "2D", "2B", "2C",
-    "2E", "3T", "3Q", "W5",
+    "H5", "CC", "2V", "2F", "2E", "3T", "3Q", "W5",
     "XX", "3P", "3R",
 )
 PORTIONS = (((X, Y, Z), 0, 1408), ((Y, Z, X), 1408, 1408), ((Z, X, Y), 2816, 1280))
 
 
-def _kernel(hid_ref, w_ref, acc, hbuf, wbuf, st_a, st_b, r_a, r_b, r_k, s_w, r_h, s_h, r_x, s_x, l_sem):
+def _kernel(hid_ref, w_ref, acc, hbuf, wbuf, st_a, st_b, r_a, r_b, r_k, s_w, r_h, s_h, r_x, l_sem):
     dp, tp = lax.axis_index("dp"), lax.axis_index("tp")
     pos, core = (dp // 4, dp % 4, tp // 2), tp % 2
 
@@ -195,7 +197,7 @@
             deliver(lambda c: st_a.at[i, :, pl.ds(c * 1024, 1024)], v, (axis, v[axis]))
         else:
             j = THREE_FLAT.index(v)
-            send(st_a.at[i], st_b.at[j], s_w.at[1], r_b.at[GROUP[v]], dev(shift(unit(axis, v[axis])), core))
+            send(st_a.at[i], st_b.at[j], s_w.at[1], r_b.at[GROUP_B[v]], dev(shift(unit(axis, v[axis])), core))
 
     def third_hop(v):
         j = THREE_FLAT.index(v)
@@ -230,14 +232,14 @@
             for v in G[which]:
                 second_hop(v)
         elif kind == "3":
-            wait(st_b.at[pl.ds(FIRST.index(G[which][0]), len(G[which]))], r_b.at[GROUP[G[which][0]]])
+            wait(st_b.at[pl.ds(FIRST.index(G[which][0]), len(G[which]))], r_b.at[GROUP_B[G[which][0]]])
             for v in G[which]:
                 third_hop(v)
         elif kind == "C":
             send(w_ref.at[:, columns(chip(pos) * 2 + 1 - core, 1)], mine, s_w.at[2], r_k.at[0], dev(pos, 1 - core))
         else:
             half = hbuf.at[pl.ds(pl.multiple_of(core * 512, 512), 512)]
-            send(half, half, s_x, r_x, dev(pos, 1 - core))
+            send(half, half, s_h, r_x, dev(pos, 1 - core))
 
     wait(hbuf.at[pl.ds(0, 512)], r_x)
 
@@ -260,8 +262,7 @@
     wait(st_a, s_w.at[0])
     wait(st_b, s_w.at[1])
     wait(wbuf.at[pl.ds(0, 127 * 32)], s_w.at[2])
-    wait(hbuf.at[pl.ds(0, 63 * 8)], s_h)
-    wait(hbuf.at[pl.ds(0, 512)], s_x)
+    wait(hbuf.at[pl.ds(0, 63 * 8 + 512)], s_h)
 
 
 def _mirror(line, core):
@@ -303,7 +304,7 @@
             scratch_shapes=[
                 pltpu.VMEM((len(FIRST), 32, 2048), jnp.bfloat16),
                 pltpu.VMEM((len(THREE_FLAT), 32, 2048), jnp.bfloat16),
-                dma((9,)), dma((4,)), dma((16,)), dma((3,)), dma((6,)), dma, dma, dma, dma,
+                dma((5,)), dma((4,)), dma((16,)), dma((3,)), dma((6,)), dma, dma, dma,
             ],
             compiler_params=pltpu.CompilerParams(collective_id=0, has_side_effects=True, vmem_limit_bytes=38 * 2**20),
         )(hid_blk, w_blk)

time: 116 us -> 116 us (level)
  no operation moved by 1% of the time
where the time goes in v6:
time: 116 us
  Pallas kernels  116 us (100%)
    pallas_call x1, Pallas kernels, local_part(): pl.pallas_call(_kernel, out_shape=[pltpu.VMEM((1024, 1024), jnp.float32),...  114 us

profile of v6, /device:TPU:1, one launch (start us, length us, event | category | flops | bytes accessed | tf_op | source)
XLA Modules:
  0.0 116.3 jit_solution(15688115433483393987)
XLA Ops:
  0.0 114.5 %shard_map.28 = (f32[1024,1024]{1,0:T(8,128)S(1)}, bf16[1024,4096]{1,0:T(8,128)(2,1)S(1)}, bf16[4096,1024]{1,0:T(8,128)(2,1)S(1)}) custom-call(bf16[8,4096]{1,0:T(8,128)(2,1)} %hid_ref.1, bf16[32,131072]{1,0:T(8,128)(2,1)} %w_ref.1), custom_call_target="tpu_custom_call" | custom-call | tf_op jit(solution)/shard_map/pallas_call | solution.py:299
  114.5 1.8 %shard_map.29 = bf16[1024,1024]{1,0:T(8,128)(2,1)} custom-call(f32[1024,1024]{1,0:T(8,128)S(1)} %get-tuple-element.8.acc, bf16[1024,4096]{1,0:T(8,128)(2,1)S(1)} %get-tuple-element.9.hbuf, bf16[4096,1024]{1,0:T(8,128)(2,1)S(1)} %get-tuple-element.10.wbuf), custom_call_target="tpu_custom_call" | custom-call | tf_op jit(solution)/shard_map/pallas_call | solution.py:312
